TPU v7x, 32 devices: a whole 2x2x4 slice. The times are simulated.
32 devices in a mesh: node: 8 (over z, x), local: 4 (over y, core).
Axes of the slice: x: 2, y: 2, z: 4, core: 2. Of those that a mesh axis runs over, the one named last changes fastest.
Arguments:
- gate_pre: bfloat16 [3584, 15360], P('node', 'local'), may hold values from -6 to 6
- up_pre: bfloat16 [3584, 15360], P('node', 'local'), may hold values from -6 to 6
- out_grad: bfloat16 [3584, 4096], P('node', 'local'), may hold values from -6 to 6
Outputs:
- weight_grad: float32 [15360, 4096], P('local', 'node')
All inputs are finite; a program needn't handle non-finite values.
Results may differ from a plain program's by a relative error of at most 0.015.
Values may be sent and summed in bfloat16 or wider, within the bound.
A program may use at most 128 MiB of HBM per device.

v0:
```python
import jax
import jax.numpy as jnp
from jax import lax
from jax.sharding import PartitionSpec as P


def shards(gate_pre, up_pre, out_grad):
    gate_float = gate_pre.astype(jnp.float32)
    activated = gate_float * jax.nn.sigmoid(gate_float)
    hidden = (activated * up_pre.astype(jnp.float32)).astype(jnp.bfloat16)
    averaging = 1.0 / lax.axis_size("node")
    partial_value = (
        lax.dot_general(
            hidden,
            lax.all_gather(out_grad, "local", axis=1, tiled=True),
            (((0,), (0,)), ((), ())),
            preferred_element_type=jnp.float32,
        )
        * averaging
    )
    shard = lax.psum_scatter(
        partial_value.astype(jnp.bfloat16), "node", scatter_dimension=1, tiled=True
    ).astype(jnp.float32)
    return shard


def solution(mesh):
    placed = (P("node", "local"), P("node", "local"), P("node", "local"))
    return jax.shard_map(
        shards, mesh=mesh, in_specs=placed, out_specs=P("local", "node"), check_vma=False
    )
```

profile of v0, /device:TPU:0, one launch (start us, length us, event | category | flops | bytes accessed | tf_op | source)
XLA Modules:
  0.0 575.0 jit_solution(17219441673584618995)
XLA Ops:
  6.5 0.0 all-gather.2.cloned.1.call-start
  6.5 0.7 all-gather.2.cloned.1.call-update
  7.3 0.0 reduce-scatter.2.cloned.1.call-start
  7.3 35.8 %all-gather.2.cloned.1.call-done = bf16[448,4096]{1,0:T(8,128)(2,1)} async-done(((bf16[448,1024]{1,0:T(8,128)(2,1)}), bf16[448,4096]{1,0:T(8,128)(2,1)}) %all-gather.2.cloned.1.call-update) | async-done | bytes 3670032 | tf_op jit(solution)/shard_map/all_gather | solution.py:15
  43.1 24.2 %multiply_convert_fusion = bf16[3840,4096]{1,0:T(8,128)(2,1)} fusion(bf16[448,4096]{1,0:T(8,128)(2,1)} %all-gather.2.cloned.1.call-done, bf16[448,3840]{1,0:T(8,128)(2,1)} %param.4, bf16[448,3840]{1,0:T(8,128)(2,1)} %param.3), kind=kOutput, calls=%fused_computation | convolution fusion | flops 14138081280 | bytes 42008576 | tf_op jit(solution)/shard_map/dot_general | solution.py:13
  67.3 0.0 reduce-scatter.2.cloned.1.call-update
  67.3 494.4 %reduce-scatter.2.cloned.1.call-done = bf16[3840,512]{1,0:T(8,128)(2,1)} async-done(((bf16[3840,4096]{1,0:T(8,128)(2,1)}), bf16[3840,512]{1,0:T(8,128)(2,1)}) %reduce-scatter.2.cloned.1.call-update) | async-done | bytes 3932176 | tf_op jit(solution)/shard_map/reduce_scatter | solution.py:21
  561.7 6.5 %convert_element_type.19 = f32[3840,512]{1,0:T(8,128)} convert(bf16[3840,512]{1,0:T(8,128)(2,1)} %reduce-scatter.2.cloned.1.call-done) | non-fusion elementwise | flops 1966080 | bytes 11796480 | tf_op jit(solution)/shard_map/convert_element_type | solution.py:23
Async XLA Ops:
  6.5 36.6 %all-gather.2.cloned.1.call-start = ((), (), s32[]{:S(2)}) async-start(), calls=%async_computation.1 | async-start | bytes 4587520 | tf_op jit(solution)/shard_map/all_gather | solution.py:15
  7.3 554.4 %reduce-scatter.2.cloned.1.call-start = ((), (), s32[]{:S(2)}) async-start(), calls=%async_computation.2 | async-start | bytes 35389440 | tf_op jit(solution)/shard_map/reduce_scatter | solution.py:21
Sparse Core Ops, SparseCore 0:
  8.9 34.1 all-gather.1
  67.4 494.2 reduce-scatter.1
where the time goes:
time: 575 us
  waiting for transfers between devices  531 us (92%)
  matrix products  24.2 us (4%)
  between operations  13.4 us (2%)
  other arithmetic  6.46 us (1%)
    reduce_scatter x1, waiting for transfers between devices, shards(): lax.psum_scatter(partial_value.astype(jnp.bfloat16), 'node', scatter_dime...  494 us
    all_gather x1, waiting for transfers between devices, shards(): lax.all_gather(out_grad, 'local', axis=1, tiled=True)  35.8 us
    dot_general x1, matrix products, shards(): lax.dot_general(hidden, lax.all_gather(out_grad, 'local', axis=1, tiled=T...  24.2 us
  transfers between devices with their start and end apart: 2, of which 2 were waited for; matrix products, arithmetic and copies ran while one was open for 0% of the time, Pallas kernels for 0%

commit v1 on v0

v1 whole, which is shorter than its diff:
```python
import functools

import jax
import jax.numpy as jnp
from jax import lax
from jax.experimental import pallas as pl
from jax.experimental.pallas import tpu as pltpu
from jax.sharding import PartitionSpec as P

WEIGHTS = (2, 4, 6, 6, 6, 4, 2)
TILE = 128


def chunks(units):
    tiles, total = units // TILE, sum(WEIGHTS)
    ends = [tiles * sum(WEIGHTS[: k + 1]) // total * TILE for k in range(len(WEIGHTS))]
    return list(zip([0] + ends[:-1], ends))


def kernel(
    n_node, n_local, hidden_ref, grad_ref, out_ref,
    whole, grads, going, coming,
    z_sem, x_sem, p_sem, g_sem, swap_sem, own_sem,
):
    wide = n_node // n_local
    halves = n_local // 2
    node, local = lax.axis_index("node"), lax.axis_index("local")
    z, x, y, c = node // wide, node % wide, local // 2, local % 2
    z_hi, z_lo = z // 2, z % 2
    units, width = out_ref.shape
    spans = chunks(units)
    count = len(spans)

    def device(z, x, y, c):
        return (z * wide + x, y * 2 + c)

    def along_x(s):
        return device(z, (x + s + wide) % wide, y, c)

    def along_z(r):
        return device((z + 2 * r + n_local) % n_local, x, y, c)

    z_pair = device(z_hi * 2 + 1 - z_lo, x, y, c)
    twin = device(z, x, y, 1 - c)

    def crossed(s, t):
        return device(
            z_hi * 2 + c, (x + s + wide) % wide, (y + t + halves) % halves, z_lo
        )

    moves = [(s, t) for t in range(halves) for s in range(wide)]
    stays = c == z_lo

    barrier = pltpu.get_barrier_semaphore()

    def greet(target):
        pl.semaphore_signal(
            barrier, inc=1, device_id=target, device_id_type=pl.DeviceIdType.MESH
        )

    greeted = [z_pair, twin, device(z_hi * 2 + 1 - z_lo, x, y, 1 - c)]
    for s in range(1, wide):
        greeted += [along_x(s), along_x(-s)]
    for r in range(1, halves):
        greeted += [along_z(r), along_z(-r)]
    for s, t in moves:
        if (s, t) != (0, 0):
            greeted += [crossed(s, t), crossed(-s, -t)]
    for target in greeted:
        greet(target)

    pl.semaphore_wait(barrier, len(greeted))

    def remote(source, target, sems, target_device):
        return pltpu.make_async_remote_copy(
            src_ref=source,
            dst_ref=target,
            send_sem=sems.at[0],
            recv_sem=sems.at[1],
            device_id=target_device,
            device_id_type=pl.DeviceIdType.MESH,
        )

    def span_of(k):
        return pl.ds(spans[k][0], spans[k][1] - spans[k][0])

    def slot(s, far):
        return hidden_ref if (s, far) == (0, 0) else whole.at[2 * s + far - 1]

    def z_copy(k):
        return remote(
            slot(0, 0).at[:, span_of(k)], slot(0, 1).at[:, span_of(k)], z_sem.at[k], z_pair
        )

    def x_copy(k, s, far):
        return remote(
            slot(0, far).at[:, span_of(k)],
            slot(s, far).at[:, span_of(k)],
            x_sem.at[k, s - 1, far],
            along_x(s),
        )

    def p_copy(k, r):
        return remote(
            going.at[r - 1, span_of(k)], coming.at[r - 1, span_of(k)],
            p_sem.at[k, r - 1], along_z(r),
        )

    def g_source(s):
        start = pl.multiple_of(((x + s) % wide) * width, 128)
        return grad_ref.at[:, pl.ds(start, width)]

    def g_copy(s, t):
        return remote(g_source(s), grads.at[t, z_lo, s], g_sem.at[t, s], crossed(s, t))

    def swap_copy(t):
        return remote(grads.at[t, c], grads.at[t, c], swap_sem.at[t], twin)

    def x_copies(k, far):
        return [x_copy(k, s, far) for s in range(1, wide)]

    def all_start(copies):
        for copy in copies:
            copy.start()

    def begin(k):
        z_copy(k).start()
        all_start(x_copies(k, 0))

    begin(0)
    own_copy = pltpu.make_async_copy(g_source(0), grads.at[0, z_lo, 0], own_sem)

    @pl.when(stays)
    def _():
        own_copy.start()

    @pl.when(jnp.logical_not(stays))
    def _():
        g_copy(0, 0).start()

    all_start([g_copy(s, t) for s, t in moves if (s, t) != (0, 0)])
    begin(1)
    z_copy(0).wait_recv()
    all_start(x_copies(0, 1))

    @pl.when(stays)
    def _():
        own_copy.wait()

    @pl.when(jnp.logical_not(stays))
    def _():
        g_copy(0, 0).wait()

    for t in range(halves):
        for s in range(wide):
            if (s, t) != (0, 0):
                g_copy(s, t).wait()
        swap_copy(t).start()
    for t in range(halves):
        swap_copy(t).wait()

    averaging = 1.0 / n_node

    def product(k, r, store):
        t = (y - z_hi - r + 2 * halves) % halves
        first, last = spans[k]

        @pl.loop(0, (last - first) // TILE)
        def _(i):
            at = pl.ds(pl.multiple_of(first + i * TILE, TILE), TILE)
            total = None
            for s in range(wide):
                for far in range(2):
                    b = z_lo if far == 0 else 1 - z_lo
                    part = lax.dot_general(
                        slot(s, far)[:, at], grads[t, b, s], (((0,), (0,)), ((), ())),
                        preferred_element_type=jnp.float32,
                    )
                    total = part if total is None else total + part
            store(at, total * averaging)

    def store_going(r):
        def store(at, value):
            going[r - 1, at, :] = value.astype(going.dtype)

        return store

    def store_out(at, value):
        out_ref[at, :] = value

    for k in range(count):
        if k + 2 < count:
            begin(k + 2)
        if k + 1 < count:
            z_copy(k + 1).wait_recv()
            all_start(x_copies(k + 1, 1))
        for copy in x_copies(k, 0) + x_copies(k, 1):
            copy.wait_recv()
        for r in range(1, halves):
            product(k, r, store_going(r))
            p_copy(k, r).start()
        product(k, 0, store_out)

    for k in range(count):
        for r in range(1, halves):
            p_copy(k, r).wait_recv()
        first, last = spans[k]

        @pl.loop(0, (last - first) // TILE)
        def _(i):
            at = pl.ds(pl.multiple_of(first + i * TILE, TILE), TILE)
            total = out_ref[at, :]
            for r in range(1, halves):
                total = total + coming[r - 1, at, :].astype(jnp.float32)
            out_ref[at, :] = total

    for k in range(count):
        z_copy(k).wait_send()
        for copy in x_copies(k, 0) + x_copies(k, 1):
            copy.wait_send()
        for r in range(1, halves):
            p_copy(k, r).wait_send()


def shards(gate_pre, up_pre, out_grad, n_node, n_local):
    wide, halves = n_node // n_local, n_local // 2
    gate_float = gate_pre.astype(jnp.float32)
    activated = gate_float * jax.nn.sigmoid(gate_float)
    hidden = (activated * up_pre.astype(jnp.float32)).astype(jnp.bfloat16)
    tokens, units = hidden.shape
    width = out_grad.shape[1] // wide
    count = len(WEIGHTS)
    return pl.pallas_call(
        functools.partial(kernel, n_node, n_local),
        out_shape=jax.ShapeDtypeStruct((units, width), jnp.float32),
        in_specs=[pl.BlockSpec(memory_space=pltpu.VMEM)] * 2,
        out_specs=pl.BlockSpec(memory_space=pltpu.VMEM),
        scratch_shapes=[
            pltpu.VMEM((2 * wide - 1, tokens, units), jnp.bfloat16),
            pltpu.VMEM((halves, 2, wide, tokens, width), jnp.bfloat16),
            pltpu.VMEM((halves - 1, units, width), jnp.bfloat16),
            pltpu.VMEM((halves - 1, units, width), jnp.bfloat16),
            pltpu.SemaphoreType.DMA((count, 2)),
            pltpu.SemaphoreType.DMA((count, wide - 1, 2, 2)),
            pltpu.SemaphoreType.DMA((count, halves - 1, 2)),
            pltpu.SemaphoreType.DMA((halves, wide, 2)),
            pltpu.SemaphoreType.DMA((halves, 2)),
            pltpu.SemaphoreType.DMA,
        ],
        compiler_params=pltpu.CompilerParams(
            collective_id=0, has_side_effects=True, vmem_limit_bytes=56 * 1024 * 1024
        ),
    )(hidden, out_grad)


def solution(mesh):
    placed = (P("node", "local"), P("node", "local"), P("node", "local"))
    return jax.shard_map(
        functools.partial(shards, n_node=mesh.shape["node"], n_local=mesh.shape["local"]),
        mesh=mesh,
        in_specs=placed,
        out_specs=P("local", "node"),
        check_vma=False,
    )
```

time: 575 us -> 259 us (0.45)
  waiting for transfers between devices: 531 us -> 0 us
  Pallas kernels: 0 us -> 246 us
  matrix products: 24.2 us -> 0 us
  between operations: 13.4 us -> 0.01 us
  local copies, waits for them, and re-layouts: 0 us -> 7.36 us
    reduce_scatter x1 -> x0, waiting for transfers between devices: 494 us -> none  [shards(): lax.psum_scatter(partial_value.astype(jnp.bfloat16), 'node', scatter_dime...]
    pallas_call x0 -> x1, Pallas kernels: none -> 246 us  [shards(): pl.pallas_call(functools.partial(kernel, n_node, n_local), out_shape=jax....]
    all_gather x1 -> x0, waiting for transfers between devices: 35.8 us -> none  [shards(): lax.all_gather(out_grad, 'local', axis=1, tiled=True)]
    dot_general x1 -> x0, matrix products: 24.2 us -> none  [shards(): lax.dot_general(hidden, lax.all_gather(out_grad, 'local', axis=1, tiled=T...]
    unnamed x0 -> x1, local copies, waits for them, and re-layouts: none -> 7.36 us
  transfers between devices with their start and end apart: 2 -> 0, of which waited for: 2 -> 0; matrix products, arithmetic and copies ran while one was open for 0% -> 0% of each run, Pallas kernels for 0% -> 0%
where the time goes in v1:
time: 259 us; the launch traced here: 258 us
  Pallas kernels  246 us (95%)
  local copies, waits for them, and re-layouts  7.36 us (3%)
  other arithmetic  5.22 us (2%)
    pallas_call x1, Pallas kernels, shards(): pl.pallas_call(functools.partial(kernel, n_node, n_local), out_shape=jax....  246 us
    unnamed x1, local copies, waits for them, and re-layouts  7.36 us
    convert_element_type x1, other arithmetic, shards(): hidden = (activated * up_pre.astype(jnp.float32)).astype(jnp.bfloat16)  5.22 us

profile of v1, /device:TPU:0, one launch (start us, length us, event | category | flops | bytes accessed | tf_op | source)
XLA Modules:
  0.0 258.5 jit_solution(6259011415928105521)
XLA Ops:
  0.0 5.2 %fusion.4.hidden_ref = bf16[448,3840]{1,0:T(8,128)(2,1)} fusion(bf16[448,3840]{1,0:T(8,128)(2,1)} %param.4, bf16[448,3840]{1,0:T(8,128)(2,1)} %param.3), kind=kLoop, calls=%fused_computation.6 | loop fusion | flops 13762560 | bytes 10321920 | tf_op jit(solution)/shard_map/convert_element_type | solution.py:229
  5.2 245.9 %shard_map.37 = f32[3840,512]{1,0:T(8,128)} custom-call(bf16[448,3840]{1,0:T(8,128)(2,1)} %fusion.4.hidden_ref, bf16[448,1024]{1,0:T(8,128)(2,1)} %grad_ref.1), custom_call_target="tpu_custom_call" | custom-call | tf_op jit(solution)/shard_map/pallas_call | solution.py:233
  251.1 7.4 %copy.5 = f32[3840,512]{1,0:T(8,128)} copy(f32[3840,512]{1,0:T(8,128)} %shard_map.37) | data formatting | bytes 15728640

commit v2 on v1

--- a/solution.py
+++ b/solution.py
@@ -7,7 +7,7 @@
 from jax.experimental.pallas import tpu as pltpu
 from jax.sharding import PartitionSpec as P
 
-WEIGHTS = (2, 4, 6, 6, 6, 4, 2)
+WEIGHTS = (1,) * 15
 TILE = 128
 
 

time: 259 us -> 234 us (0.903)
  Pallas kernels: 246 us -> 221 us
    pallas_call x1, Pallas kernels: 246 us -> 221 us  [shards(): pl.pallas_call(functools.partial(kernel, n_node, n_local), out_shape=jax....]
where the time goes in v2:
time: 234 us
  Pallas kernels  221 us (94%)
  local copies, waits for them, and re-layouts  7.36 us (3%)
  other arithmetic  5.22 us (2%)
    pallas_call x1, Pallas kernels, shards(): pl.pallas_call(functools.partial(kernel, n_node, n_local), out_shape=jax....  221 us
    unnamed x1, local copies, waits for them, and re-layouts  7.36 us
    convert_element_type x1, other arithmetic, shards(): hidden = (activated * up_pre.astype(jnp.float32)).astype(jnp.bfloat16)  5.22 us

profile of v2, /device:TPU:0, one launch (start us, length us, event | category | flops | bytes accessed | tf_op | source)
XLA Modules:
  0.0 233.8 jit_solution(10181732872682154699)
XLA Ops:
  0.0 5.2 %fusion.4.hidden_ref = bf16[448,3840]{1,0:T(8,128)(2,1)} fusion(bf16[448,3840]{1,0:T(8,128)(2,1)} %param.4, bf16[448,3840]{1,0:T(8,128)(2,1)} %param.3), kind=kLoop, calls=%fused_computation.6 | loop fusion | flops 13762560 | bytes 10321920 | tf_op jit(solution)/shard_map/convert_element_type | solution.py:229
  5.2 221.2 %shard_map.37 = f32[3840,512]{1,0:T(8,128)} custom-call(bf16[448,3840]{1,0:T(8,128)(2,1)} %fusion.4.hidden_ref, bf16[448,1024]{1,0:T(8,128)(2,1)} %grad_ref.1), custom_call_target="tpu_custom_call" | custom-call | tf_op jit(solution)/shard_map/pallas_call | solution.py:233
  226.5 7.4 %copy.5 = f32[3840,512]{1,0:T(8,128)} copy(f32[3840,512]{1,0:T(8,128)} %shard_map.37) | data formatting | bytes 15728640
